TPU v7x, 512 devices: a whole 4x8x8 slice. The times are simulated.
512 devices in a mesh: dp: 8 (over z_hi, core), mp: 64 (over z_lo, x, y).
Axes of the slice: x: 4, y: 8, z: 8 (z_hi: 4, z_lo: 2; z = z_hi * 2 + z_lo), core: 2. Of those that a mesh axis runs over, the one named last changes fastest.
Arguments:
- inputs: bfloat16 [2048, 4096], P('dp'), may hold values from -6 to 6
- upstream: bfloat16 [2048, 4096], P('dp'), may hold values from -6 to 6
- eig_tiles: bfloat16 [64, 8, 2, 128, 128], P('mp'), may hold values from -0.09375 to 0.09375
- eigvals: float32 [4096], replicated, may hold values from 0.25 to 4
Outputs:
- grad_t: bfloat16 [4096, 2048], P('mp', 'dp')
All inputs are finite; a program needn't handle non-finite values.
Results may differ from a plain program's by a relative error of at most 0.013.
Values may be sent and summed in bfloat16 or wider, within the bound.
No kernel may reach another device: no remote copies, remote signals or barrier semaphores. Data moves between devices by JAX's collectives and lax.ppermute only.
A program may use at most 64 MiB of HBM per device.

v0:
```python
import jax
import jax.numpy as jnp
from jax import lax
from jax.sharding import PartitionSpec as P


def split_up(value, dim, length):
    dims = value.shape
    blocks = value.reshape(*dims[:dim], length, dims[dim] // length, *dims[dim + 1 :])
    return jnp.moveaxis(blocks, dim, 0)


def summed_on_arrival(value, axis, dim):
    length = lax.axis_size(axis)
    blocks = lax.all_to_all(split_up(value, dim, length), axis, 0, 0, tiled=True)
    return jnp.sum(blocks.astype(jnp.float32), axis=0)


def laid_out(blocks, dim):
    blocks = jnp.moveaxis(blocks, 0, dim)
    dims = blocks.shape
    return blocks.reshape(*dims[:dim], dims[dim] * dims[dim + 1], *dims[dim + 2 :])


def copy_for_each(value, axis):
    length = lax.axis_size(axis)
    return lax.all_to_all(
        jnp.broadcast_to(value[None], (length, *value.shape)), axis, 0, 0, tiled=True
    )


def gather_directly(value, axis, dim):
    return laid_out(copy_for_each(value, axis), dim)


def kernel_of(left, right):
    root_left = jnp.sqrt(left)[:, None]
    root_right = jnp.sqrt(right)[None, :]
    return -1.0 / (root_left * root_right * (root_left + root_right))


def on_device(inputs, upstream, eig_tiles, eigvals):
    groups = lax.axis_size("mp")
    member = lax.axis_index("mp")
    width = eigvals.shape[0]
    slab = width // groups
    tile_rows = eig_tiles.shape[1]
    tile_cols = eig_tiles.shape[2]
    tile = eig_tiles.shape[3]
    grid_rows = width // (tile_rows * tile)
    grid_cols = groups // grid_rows
    piece = tile_cols * tile // groups
    local = jnp.transpose(eig_tiles[0], (0, 2, 1, 3)).reshape(tile_rows * tile, groups, piece)
    moved = lax.all_to_all(local, "mp", split_axis=1, concat_axis=1, tiled=True)
    moved = moved.reshape(tile_rows, tile, grid_rows, grid_cols, piece)
    basis = jnp.transpose(moved, (0, 2, 1, 3, 4)).reshape(width, slab)
    ordered = jnp.transpose(eigvals.reshape(tile_cols, grid_cols, tile), (1, 0, 2)).reshape(
        grid_cols, groups, piece
    )
    ordered = jnp.transpose(ordered, (1, 0, 2)).reshape(width)
    own = lax.dynamic_slice_in_dim(ordered, member * slab, slab)
    proj_in = jnp.dot(inputs, basis, preferred_element_type=jnp.float32).astype(jnp.bfloat16)
    proj_up = jnp.dot(upstream, basis, preferred_element_type=jnp.float32).astype(jnp.bfloat16)
    stacked = jnp.stack([proj_in, proj_up], 0)
    over_tokens = (((0,), (0,)), ((), ()))
    pieces = lax.all_gather(stacked, "mp", axis=2, tiled=True)
    part_in = pieces[0]
    part_up = pieces[1]
    block = lax.dot_general(proj_in, part_up, over_tokens, preferred_element_type=jnp.float32)
    block = block + lax.dot_general(
        proj_up, part_in, over_tokens, preferred_element_type=jnp.float32
    )
    joined = jnp.concatenate([block, part_in.astype(jnp.float32)], 0)
    gram = joined[:slab]
    all_in = joined[slab:].astype(jnp.bfloat16)
    share = summed_on_arrival(gram.astype(jnp.bfloat16), "dp", 0)
    count = share.shape[0]
    own_part = lax.dynamic_slice_in_dim(own, lax.axis_index("dp") * count, count)
    part = (kernel_of(own_part, ordered) * (0.5 * share)).astype(jnp.bfloat16)
    weighted = gather_directly(part, "dp", 0)
    over_columns = (((1,), (1,)), ((), ()))
    mixed = lax.dot_general(all_in, weighted, over_columns, preferred_element_type=jnp.float32)
    factor = 2.0 / (lax.axis_size("dp") * inputs.shape[0])
    update = (proj_up.astype(jnp.float32) / jnp.sqrt(own)[None, :] + factor * mixed).astype(
        jnp.bfloat16
    )
    own_rows = lax.all_to_all(basis, "mp", split_axis=0, concat_axis=1, tiled=True)
    every_update = gather_directly(update, "mp", 1)
    result = lax.dot_general(
        own_rows, every_update, over_columns, preferred_element_type=jnp.float32
    )
    return result.astype(jnp.bfloat16)


def solution(mesh):
    return jax.shard_map(
        on_device,
        mesh=mesh,
        in_specs=(P("dp", None), P("dp", None), P("mp", None, None, None, None), P()),
        out_specs=P("mp", "dp"),
        check_vma=False,
    )
```

profile of v0, /device:TPU:8, one launch (start us, length us, event | category | flops | bytes accessed | tf_op | source)
XLA Modules:
  0.0 494.4 jit_solution(2258323800576001424)
XLA Ops:
  6.5 0.0 copy-start
  6.5 0.0 all-gather.2.cloned.1.call-start
  6.5 1.5 copy.11
  8.0 0.1 reshape.93
  8.2 30.6 %all_to_all.36 = bf16[1024,64,4]{0,2,1:T(4,128)(2,1)S(1)} all-to-all(bf16[1024,64,4]{0,2,1:T(4,128)(2,1)S(1)} %reshape.93), channel_id=1, replica_groups=mesh['dp'=8,'mp'=64] {'mp'}, dimensions={1} | all-to-all | bytes 1048576 | tf_op jit(solution)/shard_map/all_to_all | solution.py:54
  38.7 1.0 reshape.102
  39.7 1.7 copy.13
  41.4 0.4 reshape.95
  41.8 0.0 copy-done
  41.8 0.0 copy-start.1
  41.8 0.8 convolution_convert_fusion.1
  42.6 0.8 copy-done.1
  43.4 0.8 convolution_convert_fusion
  44.2 0.6 pad_maximum_fusion
  44.8 0.0 all-gather.2.cloned.1.call-update
  44.8 303.2 %all-gather.2.cloned.1.call-done = bf16[2,256,4096]{1,2,0:T(8,128)(2,1)} async-done(((bf16[2,256,64]{1,2,0:T(8,128)(2,1)}), bf16[2,256,4096]{1,2,0:T(8,128)(2,1)}) %all-gather.2.cloned.1.call-update) | async-done | bytes 4194320 | tf_op jit(solution)/shard_map/all_gather | solution.py:66
  348.1 2.3 fusion.2
  350.4 0.0 copy-start.2
  350.4 3.2 fusion.1
  353.6 6.8 %all-to-all-start.1 = ((bf16[8,8,4096]{2,1,0:T(8,128)(2,1)}), bf16[8,8,4096]{2,1,0:T(8,128)(2,1)S(1)}, u32[]{:S(2)}, u32[]{:S(2)}) async-start(bf16[8,8,4096]{2,1,0:T(8,128)(2,1)} %fusion.1), calls=%async_computation.1 | async-start | bytes 1048576 | tf_op jit(solution)/shard_map/all_to_all | solution.py:15
  360.4 0.0 copy-done.2
  360.4 0.1 copy.14
  360.5 1.2 copy.15
  361.8 1.3 reshape.98
  363.1 0.1 dynamic-slice_sqrt_fusion
  363.2 15.2 %all-to-all-done.1 = bf16[8,8,4096]{2,1,0:T(8,128)(2,1)S(1)} async-done(((bf16[8,8,4096]{2,1,0:T(8,128)(2,1)}), bf16[8,8,4096]{2,1,0:T(8,128)(2,1)S(1)}, u32[]{:S(2)}, u32[]{:S(2)}) %all-to-all-start.1) | async-done | bytes 524320 | tf_op jit(solution)/shard_map/all_to_all | solution.py:15
  378.4 0.1 convert_reduce_fusion
  378.5 0.1 multiply_convert_fusion
  378.6 0.9 broadcast_in_dim.4
  379.4 3.5 all-to-all-start.2
  382.9 1.4 all_to_all.28
  384.3 2.9 copy.17
  387.3 3.0 reshape.103
  390.3 10.5 %all-to-all-done.2 = bf16[8,8,4096]{2,1,0:T(8,128)(2,1)S(1)} async-done(((bf16[8,8,4096]{2,1,0:T(8,128)(2,1)}), bf16[8,8,4096]{2,1,0:T(8,128)(2,1)S(1)}, u32[]{:S(2)}, u32[]{:S(2)}) %all-to-all-start.2) | async-done | bytes 524320 | tf_op jit(solution)/shard_map/all_to_all | solution.py:27
  400.8 8.2 %all-to-all-start.4 = ((bf16[64,2,2048]{2,1,0:T(2,128)(2,1)}), bf16[64,2,2048]{2,1,0:T(2,128)(2,1)S(1)}, u32[]{:S(2)}, u32[]{:S(2)}) async-start(bf16[64,2,2048]{2,1,0:T(2,128)(2,1)} %reshape.103), calls=%async_computation.4 | async-start | bytes 1048576 | tf_op jit(solution)/shard_map/all_to_all | solution.py:87
  409.0 0.1 dynamic-slice_sqrt_fusion.1
  409.1 2.1 fusion.11
  411.2 15.7 %all-to-all-done.4 = bf16[64,2,2048]{2,1,0:T(2,128)(2,1)S(1)} async-done(((bf16[64,2,2048]{2,1,0:T(2,128)(2,1)}), bf16[64,2,2048]{2,1,0:T(2,128)(2,1)S(1)}, u32[]{:S(2)}, u32[]{:S(2)}) %all-to-all-start.4) | async-done | bytes 524320 | tf_op jit(solution)/shard_map/all_to_all | solution.py:87
  426.9 1.6 broadcast_in_dim.5
  428.4 5.7 %all-to-all-start.3 = ((bf16[64,256,64]{1,2,0:T(8,128)(2,1)}), bf16[64,256,64]{1,2,0:T(8,128)(2,1)}, u32[]{:S(2)}, u32[]{:S(2)}) async-start(bf16[64,256,64]{1,2,0:T(8,128)(2,1)} %broadcast_in_dim.5), calls=%async_computation.3 | async-start | bytes 4194304 | tf_op jit(solution)/shard_map/all_to_all | solution.py:27
  434.2 1.6 reshape.104
  435.8 48.6 %all-to-all-done.3 = bf16[64,256,64]{1,2,0:T(8,128)(2,1)} async-done(((bf16[64,256,64]{1,2,0:T(8,128)(2,1)}), bf16[64,256,64]{1,2,0:T(8,128)(2,1)}, u32[]{:S(2)}, u32[]{:S(2)}) %all-to-all-start.3) | async-done | bytes 2097184 | tf_op jit(solution)/shard_map/all_to_all | solution.py:27
  484.5 3.0 fusion.15
  (1 shorter events, 0.0 us)
Async XLA Ops:
  6.5 35.3 %copy-start = (bf16[256,4096]{1,0:T(8,128)(2,1)S(1)}, bf16[256,4096]{1,0:T(8,128)(2,1)}, u32[]{:S(2)}) copy-start(bf16[256,4096]{1,0:T(8,128)(2,1)} %param.5) | copy-start | bytes 6291460
  6.5 341.5 %all-gather.2.cloned.1.call-start = ((), (), s32[]{:S(2)}) async-start(), calls=%async_computation.5 | async-start | bytes 4259840 | tf_op jit(solution)/shard_map/all_gather | solution.py:66
  41.8 1.6 copy-start.1
  350.4 10.0 %copy-start.2 = (f32[4096]{0:T(1024)S(1)}, f32[4096]{0:T(1024)}, u32[]{:S(2)}) copy-start(f32[4096]{0:T(1024)} %param.7) | copy-start | bytes 49156
  353.6 24.8 %all-to-all-start.1 = ((bf16[8,8,4096]{2,1,0:T(8,128)(2,1)}), bf16[8,8,4096]{2,1,0:T(8,128)(2,1)S(1)}, u32[]{:S(2)}, u32[]{:S(2)}) async-start(bf16[8,8,4096]{2,1,0:T(8,128)(2,1)} %fusion.1), calls=%async_computation.1 | async-start | bytes 1048576 | tf_op jit(solution)/shard_map/all_to_all | solution.py:15
  379.4 21.4 %all-to-all-start.2 = ((bf16[8,8,4096]{2,1,0:T(8,128)(2,1)}), bf16[8,8,4096]{2,1,0:T(8,128)(2,1)S(1)}, u32[]{:S(2)}, u32[]{:S(2)}) async-start(bf16[8,8,4096]{2,1,0:T(8,128)(2,1)} %broadcast_in_dim.4), calls=%async_computation.2 | async-start | bytes 1048576 | tf_op jit(solution)/shard_map/all_to_all | solution.py:27
  400.8 26.1 %all-to-all-start.4 = ((bf16[64,2,2048]{2,1,0:T(2,128)(2,1)}), bf16[64,2,2048]{2,1,0:T(2,128)(2,1)S(1)}, u32[]{:S(2)}, u32[]{:S(2)}) async-start(bf16[64,2,2048]{2,1,0:T(2,128)(2,1)} %reshape.103), calls=%async_computation.4 | async-start | bytes 1048576 | tf_op jit(solution)/shard_map/all_to_all | solution.py:87
  428.4 56.0 %all-to-all-start.3 = ((bf16[64,256,64]{1,2,0:T(8,128)(2,1)}), bf16[64,256,64]{1,2,0:T(8,128)(2,1)}, u32[]{:S(2)}, u32[]{:S(2)}) async-start(bf16[64,256,64]{1,2,0:T(8,128)(2,1)} %broadcast_in_dim.5), calls=%async_computation.3 | async-start | bytes 4194304 | tf_op jit(solution)/shard_map/all_to_all | solution.py:27
Sparse Core Ops, SparseCore 0:
  45.0 303.0 all-gather.1
where the time goes:
time: 495 us; the launch traced here: 494 us
  waiting for transfers between devices  393 us (79%)
  blocking collectives  30.6 us (6%)
  starting transfers between devices  24.3 us (5%)
  local copies, waits for them, and re-layouts  19.8 us (4%)
  between operations  13.5 us (3%)
  matrix products  12.1 us (2%)
    all_gather x1, waiting for transfers between devices, on_device(): pieces = lax.all_gather(stacked, 'mp', axis=2, tiled=True)  303 us
    all_to_all x2, waiting for transfers between devices, copy_for_each(): lax.all_to_all(jnp.broadcast_to(value[None], (length, *value.shape)), axi...  59.2 us
    all_to_all x1, blocking collectives, on_device(): moved = lax.all_to_all(local, 'mp', split_axis=1, concat_axis=1, tiled=True)  30.6 us
    all_to_all x1, waiting for transfers between devices, on_device(): lax.all_to_all(basis, 'mp', split_axis=0, concat_axis=1, tiled=True)  15.7 us
    all_to_all x1, waiting for transfers between devices, summed_on_arrival(): lax.all_to_all(split_up(value, dim, length), axis, 0, 0, tiled=True)  15.2 us
  transfers between devices with their start and end apart: 5, of which 5 were waited for; matrix products, arithmetic and copies ran while one was open for 3% of the time, Pallas kernels for 0%

commit v1 on v0

--- a/solution.py
+++ b/solution.py
@@ -63,7 +63,11 @@
     proj_up = jnp.dot(upstream, basis, preferred_element_type=jnp.float32).astype(jnp.bfloat16)
     stacked = jnp.stack([proj_in, proj_up], 0)
     over_tokens = (((0,), (0,)), ((), ()))
-    pieces = lax.all_gather(stacked, "mp", axis=2, tiled=True)
+
+    def begin_the_task(u, d_out):
+        return jnp.concatenate(lax.all_gather(u, "mp"), axis=d_out)
+
+    pieces = begin_the_task(stacked, 2)
     part_in = pieces[0]
     part_up = pieces[1]
     block = lax.dot_general(proj_in, part_up, over_tokens, preferred_element_type=jnp.float32)

time: 495 us -> 496 us (level)
  transfers between devices with their start and end apart: 5 -> 5, of which waited for: 5 -> 5; matrix products, arithmetic and copies ran while one was open for 3% -> 2% of each run, Pallas kernels for 0% -> 0%
where the time goes in v1:
time: 496 us; the launch traced here: 495 us
  waiting for transfers between devices  395 us (80%)
  blocking collectives  30.6 us (6%)
  starting transfers between devices  24.8 us (5%)
  local copies, waits for them, and re-layouts  21.5 us (4%)
  between operations  13.5 us (3%)
  matrix products  8.75 us (2%)
    all_gather x1, waiting for transfers between devices, begin_the_task(): return jnp.concatenate(lax.all_gather(u, 'mp'), axis=d_out)  303 us
    all_to_all x2, waiting for transfers between devices, copy_for_each(): lax.all_to_all(jnp.broadcast_to(value[None], (length, *value.shape)), axi...  60.7 us
    all_to_all x1, blocking collectives, on_device(): moved = lax.all_to_all(local, 'mp', split_axis=1, concat_axis=1, tiled=True)  30.6 us
    all_to_all x1, waiting for transfers between devices, on_device(): lax.all_to_all(basis, 'mp', split_axis=0, concat_axis=1, tiled=True)  16 us
    all_to_all x1, waiting for transfers between devices, summed_on_arrival(): lax.all_to_all(split_up(value, dim, length), axis, 0, 0, tiled=True)  15.5 us
  transfers between devices with their start and end apart: 5, of which 5 were waited for; matrix products, arithmetic and copies ran while one was open for 2% of the time, Pallas kernels for 0%

profile of v1, /device:TPU:8, one launch (start us, length us, event | category | flops | bytes accessed | tf_op | source)
XLA Modules:
  0.0 495.2 jit_solution(15396127786331049673)
XLA Ops:
  6.5 0.0 copy-start
  6.5 0.0 all-gather.3.cloned.1.call-start
  6.5 1.5 copy.18
  8.0 0.1 reshape.101
  8.2 30.6 %all_to_all.36 = bf16[1024,64,4]{0,2,1:T(4,128)(2,1)S(1)} all-to-all(bf16[1024,64,4]{0,2,1:T(4,128)(2,1)S(1)} %reshape.101), channel_id=1, replica_groups=mesh['dp'=8,'mp'=64] {'mp'}, dimensions={1} | all-to-all | bytes 1048576 | tf_op jit(solution)/shard_map/all_to_all | solution.py:54
  38.7 1.0 reshape.112
  39.7 1.7 copy.20
  41.4 0.4 reshape.103
  41.8 0.0 copy-done
  41.8 0.0 copy-start.3
  41.8 0.8 convolution_convert_fusion.1
  42.6 0.8 copy-done.3
  43.4 0.8 convolution_convert_fusion
  44.2 0.6 pad_maximum_fusion
  44.8 0.0 all-gather.3.cloned.1.call-update
  44.8 303.0 %all-gather.3.cloned.1.call-done = bf16[128,256,64]{1,2,0:T(8,128)(2,1)} async-done(((bf16[2,256,64]{1,2,0:T(8,128)(2,1)}), bf16[128,256,64]{1,2,0:T(8,128)(2,1)}) %all-gather.3.cloned.1.call-update) | async-done | bytes 4194320 | tf_op jit(solution)/shard_map/all_gather | solution.py:68
  347.9 2.7 fusion.17
  350.6 0.0 copy-start.1
  350.6 0.7 fusion.18
  351.4 0.6 copy-done.1
  352.0 0.0 copy-start.4
  352.0 1.6 fusion.1
  353.5 6.8 %all-to-all-start.1 = ((bf16[8,8,4096]{2,1,0:T(8,128)(2,1)}), bf16[8,8,4096]{2,1,0:T(8,128)(2,1)S(1)}, u32[]{:S(2)}, u32[]{:S(2)}) async-start(bf16[8,8,4096]{2,1,0:T(8,128)(2,1)} %fusion.1), calls=%async_computation.1 | async-start | bytes 1048576 | tf_op jit(solution)/shard_map/all_to_all | solution.py:15
  360.3 0.0 copy-done.4
  360.3 0.1 copy.21
  360.4 1.2 copy.22
  361.7 1.3 reshape.106
  363.0 0.1 dynamic-slice_sqrt_fusion
  363.1 15.5 %all-to-all-done.1 = bf16[8,8,4096]{2,1,0:T(8,128)(2,1)S(1)} async-done(((bf16[8,8,4096]{2,1,0:T(8,128)(2,1)}), bf16[8,8,4096]{2,1,0:T(8,128)(2,1)S(1)}, u32[]{:S(2)}, u32[]{:S(2)}) %all-to-all-start.1) | async-done | bytes 524320 | tf_op jit(solution)/shard_map/all_to_all | solution.py:15
  378.6 0.1 convert_reduce_fusion
  378.6 0.1 multiply_convert_fusion
  378.7 0.8 broadcast_in_dim.4
  379.6 4.1 all-to-all-start.2
  383.7 1.4 all_to_all.28
  385.1 2.2 copy.24
  387.3 1.5 reshape.113
  388.9 12.6 %all-to-all-done.2 = bf16[8,8,4096]{2,1,0:T(8,128)(2,1)} async-done(((bf16[8,8,4096]{2,1,0:T(8,128)(2,1)}), bf16[8,8,4096]{2,1,0:T(8,128)(2,1)}, u32[]{:S(2)}, u32[]{:S(2)}) %all-to-all-start.2) | async-done | bytes 524320 | tf_op jit(solution)/shard_map/all_to_all | solution.py:27
  401.5 8.1 %all-to-all-start.4 = ((bf16[64,2,2048]{2,1,0:T(2,128)(2,1)}), bf16[64,2,2048]{2,1,0:T(2,128)(2,1)S(1)}, u32[]{:S(2)}, u32[]{:S(2)}) async-start(bf16[64,2,2048]{2,1,0:T(2,128)(2,1)} %reshape.113), calls=%async_computation.4 | async-start | bytes 1048576 | tf_op jit(solution)/shard_map/all_to_all | solution.py:91
  409.6 0.1 dynamic-slice_sqrt_fusion.1
  409.7 2.2 fusion.8
  411.9 16.0 %all-to-all-done.4 = bf16[64,2,2048]{2,1,0:T(2,128)(2,1)S(1)} async-done(((bf16[64,2,2048]{2,1,0:T(2,128)(2,1)}), bf16[64,2,2048]{2,1,0:T(2,128)(2,1)S(1)}, u32[]{:S(2)}, u32[]{:S(2)}) %all-to-all-start.4) | async-done | bytes 524320 | tf_op jit(solution)/shard_map/all_to_all | solution.py:91
  427.9 0.0 copy-start.2
  427.9 1.6 broadcast_in_dim.5
  429.4 0.0 copy-done.2
  429.5 5.8 %all-to-all-start.3 = ((bf16[64,256,64]{1,2,0:T(8,128)(2,1)}), bf16[64,256,64]{1,2,0:T(8,128)(2,1)}, u32[]{:S(2)}, u32[]{:S(2)}) async-start(bf16[64,256,64]{1,2,0:T(8,128)(2,1)} %broadcast_in_dim.5), calls=%async_computation.3 | async-start | bytes 4194304 | tf_op jit(solution)/shard_map/all_to_all | solution.py:27
  435.2 2.3 reshape.114
  437.5 48.1 %all-to-all-done.3 = bf16[64,256,64]{1,2,0:T(8,128)(2,1)} async-done(((bf16[64,256,64]{1,2,0:T(8,128)(2,1)}), bf16[64,256,64]{1,2,0:T(8,128)(2,1)}, u32[]{:S(2)}, u32[]{:S(2)}) %all-to-all-start.3) | async-done | bytes 2097184 | tf_op jit(solution)/shard_map/all_to_all | solution.py:27
  485.6 2.7 fusion.12
  (1 shorter events, 0.0 us)
Async XLA Ops:
  6.5 35.3 %copy-start = (bf16[256,4096]{1,0:T(8,128)(2,1)S(1)}, bf16[256,4096]{1,0:T(8,128)(2,1)}, u32[]{:S(2)}) copy-start(bf16[256,4096]{1,0:T(8,128)(2,1)} %param.5) | copy-start | bytes 6291460
  6.5 341.3 %all-gather.3.cloned.1.call-start = ((), (), s32[]{:S(2)}) async-start(), calls=%async_computation.5 | async-start | bytes 4259840 | tf_op jit(solution)/shard_map/all_gather | solution.py:68
  41.8 1.6 copy-start.3
  350.6 1.3 copy-start.1
  352.0 8.3 %copy-start.4 = (f32[4096]{0:T(1024)S(1)}, f32[4096]{0:T(1024)}, u32[]{:S(2)}) copy-start(f32[4096]{0:T(1024)} %param.7) | copy-start | bytes 49156
  353.5 25.0 %all-to-all-start.1 = ((bf16[8,8,4096]{2,1,0:T(8,128)(2,1)}), bf16[8,8,4096]{2,1,0:T(8,128)(2,1)S(1)}, u32[]{:S(2)}, u32[]{:S(2)}) async-start(bf16[8,8,4096]{2,1,0:T(8,128)(2,1)} %fusion.1), calls=%async_computation.1 | async-start | bytes 1048576 | tf_op jit(solution)/shard_map/all_to_all | solution.py:15
  379.6 21.9 %all-to-all-start.2 = ((bf16[8,8,4096]{2,1,0:T(8,128)(2,1)}), bf16[8,8,4096]{2,1,0:T(8,128)(2,1)}, u32[]{:S(2)}, u32[]{:S(2)}) async-start(bf16[8,8,4096]{2,1,0:T(8,128)(2,1)} %broadcast_in_dim.4), calls=%async_computation.2 | async-start | bytes 1048576 | tf_op jit(solution)/shard_map/all_to_all | solution.py:27
  401.5 26.4 %all-to-all-start.4 = ((bf16[64,2,2048]{2,1,0:T(2,128)(2,1)}), bf16[64,2,2048]{2,1,0:T(2,128)(2,1)S(1)}, u32[]{:S(2)}, u32[]{:S(2)}) async-start(bf16[64,2,2048]{2,1,0:T(2,128)(2,1)} %reshape.113), calls=%async_computation.4 | async-start | bytes 1048576 | tf_op jit(solution)/shard_map/all_to_all | solution.py:91
  427.9 1.6 copy-start.2
  429.5 56.2 %all-to-all-start.3 = ((bf16[64,256,64]{1,2,0:T(8,128)(2,1)}), bf16[64,256,64]{1,2,0:T(8,128)(2,1)}, u32[]{:S(2)}, u32[]{:S(2)}) async-start(bf16[64,256,64]{1,2,0:T(8,128)(2,1)} %broadcast_in_dim.5), calls=%async_computation.3 | async-start | bytes 4194304 | tf_op jit(solution)/shard_map/all_to_all | solution.py:27
Sparse Core Ops, SparseCore 0:
  45.0 302.8 all-gather.2
